TPU v7x, 128 devices: a whole 4x4x4 slice. The times are simulated.
128 devices in a mesh: traj: 8 (over z, y_hi), lon: 16 (over y_lo, x, core).
Axes of the slice: x: 4, y: 4 (y_hi: 2, y_lo: 2; y = y_hi * 2 + y_lo), z: 4, core: 2. Of those that a mesh axis runs over, the one named last changes fastest.
Arguments:
- states: float32 [8, 78, 16, 2048], P('traj', None, None, 'lon')
- obs_index: int32 [8, 4096], P('traj', 'lon'), may hold values from 0 to 32767, as said below
- obs_values: float32 [8, 78, 4096], P('traj', None, 'lon'), may hold values from -8 to 8
- first_weight: bfloat16 [256, 2106], replicated, may hold values from -0.125 to 0.125
- first_bias: float32 [256], replicated, may hold values from -4 to 4
- second_weight: bfloat16 [234, 2304], replicated, may hold values from -0.125 to 0.125
Outputs:
- updated: float32 [8, 78, 16, 2048], P('traj', None, None, 'lon')
Inputs may be any that keep to these rules, and one draw needn't show every extreme that they name: Entries k of obs_index[t] with k // 256 = j lie in longitude columns j * 128 to (j + 1) * 128 - 1; the cells of one state are distinct.
All inputs are finite; a program needn't handle non-finite values.
Results may differ from a plain program's by a relative error of at most 0.0028.
Values may be sent and summed in bfloat16 or wider, within the bound.
No kernel may reach another device: no remote copies, remote signals or barrier semaphores. Data moves between devices by JAX's collectives and lax.ppermute only.
A program may use at most 128 MiB of HBM per device.

v0:
```python
import functools

import jax
import jax.numpy as jnp
from jax import lax
from jax.experimental import pallas as pl
from jax.experimental.pallas import tpu as pltpu
from jax.sharding import Mesh
from jax.sharding import PartitionSpec as P

STEPS = 2
LON = ("lon_0", "lon_1", "lon_2")
TRAJ = ("traj_0", "traj_1")
ALL = TRAJ + LON
LANES = 128
F32 = jnp.float32
BF16 = jnp.bfloat16
VMEM = pl.BlockSpec(memory_space=pltpu.VMEM)


def call(kernel, outs, scratch, *args):
    return pl.pallas_call(
        kernel,
        out_shape=outs,
        in_specs=[VMEM] * len(args),
        out_specs=[VMEM] * len(outs),
        scratch_shapes=scratch,
        compiler_params=pltpu.CompilerParams(vmem_limit_bytes=48 * 2**20),
        name=kernel.func.__name__ if isinstance(kernel, functools.partial) else kernel.__name__,
    )(*args)


def iota(shape, dim):
    return lax.broadcasted_iota(jnp.int32, shape, dim)


def prepare_kernel(nvar, x_ref, index_ref, values_ref, send_ref, base_ref, sums_ref, xs, xf, vs):
    lines, cols = x_ref.shape
    rows = lines // nvar
    xs[...] = jnp.zeros_like(xs)
    xs[:lines, :] = x_ref[...]
    vpad = xs.shape[0] // rows
    for r in range(rows):
        picked = xs[pl.ds(r, vpad, stride=rows), :]
        picked = jnp.concatenate([picked, jnp.zeros((LANES - vpad, cols), F32)], 0)
        xf[pl.ds(r, cols, stride=rows), :] = picked.T
    vs[...] = jnp.zeros_like(vs)
    vs[:, :nvar] = values_ref[...]
    turned = vs[...]
    high = turned.astype(BF16)
    rest = turned - high.astype(F32)
    middle = rest.astype(BF16)
    low = (rest - middle.astype(F32)).astype(BF16)
    table = jnp.concatenate([high, middle, low, jnp.ones_like(high)], 1)
    index = index_ref[...]
    place = (index % LANES) * rows + index // (16 * LANES)
    chunk = 256
    nobs = index.shape[1]

    def one(i, acc):
        at = pl.ds(i * chunk, chunk)
        x = xf[at, :]
        cell = iota((chunk, nobs), 0) + i * chunk
        picks = jnp.where(cell == place, 1.0, 0.0).astype(BF16)
        found = jnp.dot(picks, table, preferred_element_type=F32)
        obs = (found[:, :LANES] + found[:, LANES : 2 * LANES]) + found[:, 2 * LANES : 3 * LANES]
        keep = 1.0 - 0.5 * found[:, 3 * LANES :]
        lane = iota((chunk, LANES), 1)
        coarse = x.astype(BF16).astype(F32)
        fine = pltpu.roll(x - coarse, nvar, 1)
        again = pltpu.roll(fine, nvar, 1)
        state = jnp.where(lane < nvar, coarse, fine)
        seen = jnp.where(lane < nvar, obs, jnp.where(lane == LANES - 1, keep, again))
        out = pl.ds(i * (chunk // rows), chunk // rows)
        send_ref[out, :rows] = state.astype(BF16).reshape(chunk // rows, rows, LANES)
        send_ref[out, rows:] = seen.astype(BF16).reshape(chunk // rows, rows, LANES)
        base_ref[out] = (keep * keep * x + (keep + 1.0) * 0.5 * obs).reshape(chunk // rows, rows, LANES)
        return acc + jnp.sum((x * x).reshape(chunk // 8, 8, LANES), 0)

    acc = lax.fori_loop(0, cols * rows // chunk, one, jnp.zeros((8, LANES), F32))
    sums_ref[...] = jnp.broadcast_to(jnp.sum(acc, 0, keepdims=True), sums_ref.shape)


def weights_kernel(nvar, w1_ref, w2_ref, w1t_ref, w2t_ref, pad, flat):
    hid = w1_ref.shape[1]
    win = 3 * nvar
    rest = jnp.zeros((hid, hid - win), F32)
    flat[...] = w1_ref[...].astype(F32)
    pad[...] = jnp.zeros_like(pad)
    for d in range(3):
        for b in range(3):
            for a in range(3):
                at = (3 * a + b) * win + d * nvar
                pad[a * nvar : (a + 1) * nvar, :] = flat[at : at + nvar, :]
            w1t_ref[pl.ds((3 * d + b) * hid, hid), :] = pad[...].astype(BF16)
    for b in range(3):
        turned = []
        for a in range(3):
            pad[:win, :] = w2_ref[:, (3 * a + b) * hid : (3 * a + b + 1) * hid].astype(F32)
            turned.append(pad[...].T)
        for d in range(3):
            parts = [t[:, (2 - d) * nvar : (3 - d) * nvar] for t in turned]
            block = jnp.concatenate(parts + [rest], 1)
            w2t_ref[pl.ds((3 * d + b) * hid, hid), :] = block.astype(BF16)


def assemble_kernel(reach, x_ref, left_ref, right_ref, out_ref):
    parts = out_ref.shape[0]
    cols = x_ref.shape[0]
    each = cols // parts
    for k in range(parts):
        first, last = k * each - reach, (k + 1) * each + reach
        lo, hi = max(first, 0), min(last, cols)
        out_ref[k, lo - first : hi - first] = x_ref[lo:hi]
        if first < 0:
            out_ref[k, :-first] = left_ref[...]
        if last > cols:
            out_ref[k, hi - first :] = right_ref[...]


def moved(value, by, edge):
    row = iota(value.shape, 0) % 16
    return jnp.where(row == edge, 0.0, pltpu.roll(value, by % value.shape[0], 0))


def convolutions(nvar, read, parts_ref, w1_ref, bias_ref, w2_ref, window, hidden, count, write):
    states, cols = window.shape[0] - 2, window.shape[1]
    rows = window.shape[2]
    inner = hidden.shape[1]
    outer = inner - 2
    total = jnp.sum(parts_ref[...], 0, keepdims=True)
    scale = 1.0 / jnp.sqrt(total / count + 1e-06)
    for edge in (0, states + 1):
        window[edge] = jnp.zeros(window.shape[1:], BF16)
        hidden[edge] = jnp.zeros(hidden.shape[1:], BF16)

    def fill(t, _):
        normed = read(t) * scale
        lane = iota(normed.shape, 1)
        mid = pltpu.roll(normed, nvar, 1)
        low = jnp.where(lane < nvar, moved(normed, 1, 0), mid)
        high = pltpu.roll(moved(normed, -1, 15), 2 * nvar - LANES, 1)
        high = jnp.where(lane < 2 * nvar - LANES, mid, high)
        window[t + 1] = jnp.concatenate([low, high], 1).astype(BF16).reshape(cols, rows, 2 * LANES)
        return 0

    lax.fori_loop(0, states, fill, 0)

    def first(t, _):
        patches = [
            window[t + d, b : b + inner].reshape(inner * rows, 2 * LANES) for d in range(3) for b in range(3)
        ]
        value = jnp.dot(jnp.concatenate(patches, 1), w1_ref[...], preferred_element_type=F32)
        value = 0.5 * (value + bias_ref[...])
        value = value * (1.0 + jnp.tanh(value))
        hidden[t + 1] = value.astype(BF16).reshape(inner, rows, value.shape[1])
        return 0

    lax.fori_loop(0, states, first, 0)

    def second(t, carry):
        patches = [
            hidden[t + d, b : b + outer].reshape(outer * rows, 2 * LANES) for d in range(3) for b in range(3)
        ]
        value = jnp.dot(jnp.concatenate(patches, 1), w2_ref[...], preferred_element_type=F32)
        low, high = value[:, :LANES], value[:, LANES:]
        lane = iota(low.shape, 1)
        mid = pltpu.roll(jnp.where(lane >= nvar, low, high), LANES - nvar, 1)
        end = pltpu.roll(high, 2 * LANES - 2 * nvar, 1)
        score = moved(low, 1, 0) + mid + moved(end, -1, 15)
        return write(t, jnp.where(lane < nvar, score, 0.0), carry)

    return lax.fori_loop(0, states, second, jnp.zeros((8, LANES), F32))


def first_step_kernel(nvar, count, s_ref, parts_ref, w1_ref, bias_ref, w2_ref, x_ref, d_ref, sums_ref, window, hidden):
    rows = s_ref.shape[2] // 2
    wide = window.shape[1]
    outer = x_ref.shape[1]
    core = d_ref.shape[1]
    skip = (outer - core) // 2
    ring = (wide - outer) // 2

    def read(t):
        state = s_ref[t, :, :rows].astype(F32).reshape(wide * rows, LANES)
        seen = s_ref[t, :, rows:].astype(F32).reshape(wide * rows, LANES)
        lane = iota(state.shape, 1)
        left = LANES - nvar
        fine = jnp.where(lane < left, pltpu.roll(state, left, 1), pltpu.roll(seen, 2 * left, 1))
        x = jnp.where(lane < nvar, state + fine, 0.0)
        mixed = (seen[:, LANES - 1 :] * x + 0.5 * seen).reshape(wide, rows, LANES)
        x_ref[t] = mixed[ring : ring + outer]
        return x

    def write(t, score, acc):
        mixed = x_ref[t].reshape(outer * rows, LANES)
        keep = s_ref[t, ring : ring + outer, rows:].astype(F32).reshape(outer * rows, LANES)[:, LANES - 1 :]
        half = 0.5 * score
        lane = iota(score.shape, 1)
        x = jnp.where(lane < nvar, mixed + half, 0.0)
        x_ref[t] = x.reshape(outer, rows, LANES)
        d_ref[t] = (keep * half).reshape(outer, rows, LANES)[skip : skip + core]
        own = x.reshape(outer, rows, LANES)[skip : skip + core]
        return acc + jnp.sum((own * own).reshape(core * rows // 8, 8, LANES), 0)

    acc = convolutions(nvar, read, parts_ref, w1_ref, bias_ref, w2_ref, window, hidden, count, write)
    sums_ref[...] = jnp.broadcast_to(jnp.sum(acc, 0, keepdims=True), sums_ref.shape)


def second_step_kernel(nvar, count, x_ref, d_ref, parts_ref, w1_ref, bias_ref, w2_ref, out_ref, window, hidden):
    wide, rows = x_ref.shape[1], x_ref.shape[2]
    core = d_ref.shape[1]

    def read(t):
        return x_ref[t].reshape(wide * rows, LANES)

    def write(t, score, acc):
        d = d_ref[t].reshape(core * rows, LANES) + 0.5 * score
        coarse = d.astype(BF16).astype(F32)
        lane = iota(d.shape, 1)
        d = jnp.where(lane < nvar, coarse, pltpu.roll(d - coarse, nvar, 1))
        out_ref[t] = d.astype(BF16).reshape(core, rows, LANES)
        return acc

    convolutions(nvar, read, parts_ref, w1_ref, bias_ref, w2_ref, window, hidden, count, write)


def finish_kernel(nvar, d_ref, base_ref, out_ref, both):
    cols, rows, _ = base_ref.shape
    d = d_ref[...].astype(F32).reshape(cols * rows, LANES)
    left = LANES - nvar
    fine = jnp.where(iota(d.shape, 1) < left, pltpu.roll(d, left, 1), 0.0)
    both[...] = base_ref[...].reshape(cols * rows, LANES) + d + fine
    for r in range(rows):
        turned = both[pl.ds(r, cols, stride=rows), :].T
        out_ref[pl.ds(r, nvar, stride=rows), :] = turned[:nvar]


def exchanged(rows, axes):
    return lax.all_to_all(rows[:, None, :], axes, 0, 0)[:, 0, :]


def body(states, obs_index, obs_values, first_weight, first_bias, second_weight):
    _, nvar, rows, cols = states.shape
    hid = first_weight.shape[0]
    parts = lax.axis_size(TRAJ)
    bands = lax.axis_size(LON)
    count = float(parts * bands * rows * cols)
    each = cols // parts
    vpad = -(-nvar // 8) * 8
    sds = jax.ShapeDtypeStruct
    everyone = sds((parts * bands, LANES), F32)
    band = (cols, rows, LANES)
    packed, base, sums = call(
        functools.partial(prepare_kernel, nvar),
        [sds((cols, 2 * rows, LANES), BF16), sds(band, F32), everyone],
        [
            pltpu.VMEM((vpad * rows, cols), F32),
            pltpu.VMEM((cols * rows, LANES), F32),
            pltpu.VMEM((obs_index.shape[1], LANES), F32),
        ],
        states.reshape(nvar * rows, cols),
        obs_index,
        obs_values[0].T,
    )
    wide = 2 * STEPS
    up = [(i, (i + 1) % bands) for i in range(bands)]
    down = [(j, i) for i, j in up]
    left = lax.ppermute(packed[cols - wide :], LON, up)
    right = lax.ppermute(packed[:wide], LON, down)
    w1, w2 = call(
        functools.partial(weights_kernel, nvar),
        [sds((9 * hid, hid), BF16), sds((9 * hid, hid), BF16)],
        [pltpu.VMEM((hid, hid), F32), pltpu.VMEM(first_weight.shape[::-1], F32)],
        first_weight.T,
        second_weight,
    )
    bias = first_bias[None]
    (sent,) = call(
        functools.partial(assemble_kernel, wide),
        [sds((parts, each + 2 * wide, 2 * rows, LANES), BF16)],
        [],
        packed,
        left,
        right,
    )
    got = lax.all_to_all(sent, TRAJ, 0, 0)
    x1, d1, sums1 = call(
        functools.partial(first_step_kernel, nvar, count),
        [sds((parts, each + 4, rows, LANES), F32), sds((parts, each, rows, LANES), F32), everyone],
        [pltpu.VMEM((parts + 2, each + 8, rows, hid), BF16), pltpu.VMEM((parts + 2, each + 6, rows, hid), BF16)],
        got,
        exchanged(sums, ALL),
        w1,
        bias,
        w2,
    )
    (d2,) = call(
        functools.partial(second_step_kernel, nvar, count),
        [sds((parts, each, rows, LANES), BF16)],
        [pltpu.VMEM((parts + 2, each + 4, rows, hid), BF16), pltpu.VMEM((parts + 2, each + 2, rows, hid), BF16)],
        x1,
        d1,
        exchanged(sums1, ALL),
        w1,
        bias,
        w2,
    )
    back = lax.all_to_all(d2, TRAJ, 0, 0)
    (out,) = call(
        functools.partial(finish_kernel, nvar),
        [sds((nvar * rows, cols), F32)],
        [pltpu.VMEM((cols * rows, LANES), F32)],
        back.reshape(cols, rows, LANES),
        base,
    )
    return out.reshape(states.shape)


def solution(mesh):
    torus = Mesh(
        mesh.devices.reshape(4, 2, 2, 4, 2), ("traj_0", "traj_1", "lon_0", "lon_1", "lon_2")
    )
    placed = (P(TRAJ, None, None, LON), P(TRAJ, LON), P(TRAJ, None, LON), P(), P(), P())
    return jax.shard_map(
        body, mesh=torus, in_specs=placed, out_specs=P(TRAJ, None, None, LON), check_vma=False
    )
```

profile of v0, /device:TPU:0, one launch (start us, length us, event | category | flops | bytes accessed | tf_op | source)
XLA Modules:
  0.0 109.0 jit_solution(14996642365146060598)
XLA Ops:
  0.0 1.0 copy.8
  1.0 0.0 copy-start.4
  1.0 1.1 copy-done.4
  2.1 0.0 copy-start.6
  2.1 0.7 copy-done.6
  2.8 3.1 %prepare_kernel.1 = (bf16[128,32,128]{2,1,0:T(8,128)(2,1)S(1)}, f32[128,16,128]{2,1,0:T(8,128)S(1)}, f32[128,128]{1,0:T(8,128)}) custom-call(f32[1248,128]{1,0:T(8,128)S(1)} %bitcast.18, s32[1,256]{1,0:T(1,128)S(1)} %copy-done.6, f32[256,78]{1,0:T(8,128)S(1)} %bitcast.19), custom_call_target="tpu_custom_call" | custom-call | tf_op jit(solution)/shard_map/prepare_kernel/pallas_call | solution.py:22
  5.9 0.0 copy-start.2
  5.9 1.0 copy-done.2
  6.9 11.2 %all-to-all-start.1 = ((f32[128,1,128]{2,1,0:T(1,128)}), f32[128,1,128]{2,1,0:T(1,128)S(1)}, u32[]{:S(2)}, u32[]{:S(2)}) async-start(f32[128,1,128]{2,1,0:T(1,128)} %bitcast.4), calls=%async_computation.1 | async-start | bytes 131072 | tf_op jit(solution)/shard_map/all_to_all | solution.py:240
  18.1 2.9 %collective-permute-start.1 = (bf16[4,32,128]{2,1,0:T(8,128)(2,1)S(1)}, bf16[4,32,128]{2,1,0:T(8,128)(2,1)S(1)}, u32[]{:S(2)}, u32[]{:S(2)}) collective-permute-start(bf16[4,32,128]{2,1,0:T(8,128)(2,1)S(1)} %get-tuple-element.21), channel_id=1, source_target_pairs={{1,0},{2,1},{3,2},{4,3},{5,4},{6,5},{7,6},{8,7},{9,8},{10,9},{11,1... | collective-permute-start | bytes 98312 | tf_op jit(solution)/shard_map/ppermute | solution.py:270
  20.9 0.0 collective-permute-start
  20.9 1.6 %collective-permute-done.1.right_ref = bf16[4,32,128]{2,1,0:T(8,128)(2,1)S(1)} collective-permute-done((bf16[4,32,128]{2,1,0:T(8,128)(2,1)S(1)}, bf16[4,32,128]{2,1,0:T(8,128)(2,1)S(1)}, u32[]{:S(2)}, u32[]{:S(2)}) %collective-permute-start.1) | collective-permute-done | bytes 32800 | tf_op jit(solution)/shard_map/ppermute | solution.py:270
  22.5 3.9 %collective-permute-done.left_ref = bf16[4,32,128]{2,1,0:T(8,128)(2,1)S(1)} collective-permute-done((bf16[4,32,128]{2,1,0:T(8,128)(2,1)S(1)}, bf16[4,32,128]{2,1,0:T(8,128)(2,1)S(1)}, u32[]{:S(2)}, u32[]{:S(2)}) %collective-permute-start) | collective-permute-done | bytes 32800 | tf_op jit(solution)/shard_map/ppermute | solution.py:269
  26.4 1.3 %assemble_kernel.1 = bf16[8,24,32,128]{3,2,1,0:T(8,128)(2,1)} custom-call(bf16[128,32,128]{2,1,0:T(8,128)(2,1)S(1)} %get-tuple-element.13.x_ref, bf16[4,32,128]{2,1,0:T(8,128)(2,1)S(1)} %collective-permute-done.left_ref, bf16[4,32,128]{2,1,0:T(8,128)(2,1)S(1)} %collective-permute-done.1.right_ref), custom_call_target="tpu_custom_call" | custom-call | tf_op jit(solution)/shard_map/assemble_kernel/pallas_call | solution.py:22
  27.7 0.0 copy-start
  27.7 0.0 all-to-all-done.1
  27.7 7.1 %all-to-all-start = ((bf16[8,24,32,128]{3,2,1,0:T(8,128)(2,1)}), bf16[8,24,32,128]{3,2,1,0:T(8,128)(2,1)}, u32[]{:S(2)}, u32[]{:S(2)}) async-start(bf16[8,24,32,128]{3,2,1,0:T(8,128)(2,1)} %assemble_kernel.1), calls=%async_computation | async-start | bytes 3145728 | tf_op jit(solution)/shard_map/all_to_all | solution.py:287
  34.8 0.0 copy-start.5
  34.8 0.0 copy-done
  34.8 0.0 copy-start.1
  34.9 1.2 %copy-done.1 = bf16[256,2106]{0,1:T(8,128)(2,1)S(1)} copy-done((bf16[256,2106]{0,1:T(8,128)(2,1)S(1)}, bf16[256,2106]{0,1:T(8,128)(2,1)}, u32[]{:S(2)}) %copy-start.1) | copy-done | bytes 1078296
  36.1 1.1 %weights_kernel.1 = (bf16[2304,256]{1,0:T(8,128)(2,1)S(1)}, bf16[2304,256]{1,0:T(8,128)(2,1)S(1)}) custom-call(bf16[2106,256]{1,0:T(8,128)(2,1)S(1)} %bitcast.17, bf16[234,2304]{1,0:T(8,128)(2,1)S(1)} %copy-done), custom_call_target="tpu_custom_call" | custom-call | tf_op jit(solution)/shard_map/weights_kernel/pallas_call | solution.py:22
  37.2 17.5 %all-to-all-done.s_ref = bf16[8,24,32,128]{3,2,1,0:T(8,128)(2,1)} async-done(((bf16[8,24,32,128]{3,2,1,0:T(8,128)(2,1)}), bf16[8,24,32,128]{3,2,1,0:T(8,128)(2,1)}, u32[]{:S(2)}, u32[]{:S(2)}) %all-to-all-start) | async-done | bytes 1572896 | tf_op jit(solution)/shard_map/all_to_all | solution.py:287
  54.6 0.0 copy-done.5
  54.6 13.5 %first_step_kernel.1 = (f32[8,20,16,128]{3,2,1,0:T(8,128)S(1)}, f32[8,16,16,128]{3,2,1,0:T(8,128)S(1)}, f32[128,128]{1,0:T(8,128)S(1)}) custom-call(bf16[8,24,32,128]{3,2,1,0:T(8,128)(2,1)} %all-to-all-done.s_ref, f32[128,128]{1,0:T(8,128)S(1)} %bitcast.20, bf16[2304,256]{1,0:T(8,128)(2,1)S(1)} %get-tuple-element.15.w1_ref, f32[1,256]{1,0:T(1,128)S(1)} %bitcast.23, ...), custom_call_target="tpu_custom_call" | custom-call | tf_op jit(solution)/shard_map/first_step_kernel/pallas_call | solution.py:22
  68.1 14.5 %all_to_all.20 = f32[128,1,128]{2,1,0:T(1,128)S(1)} all-to-all(f32[128,1,128]{2,1,0:T(1,128)S(1)} %bitcast.22), channel_id=1, replica_groups=mesh['traj_0'=4,'traj_1'=2,'lon_0'=2,'lon_1'=4,'lon_2'=2] {'traj_0','tra..., dimensions={0} | all-to-all | bytes 131072 | tf_op jit(solution)/shard_map/all_to_all | solution.py:240
  82.6 10.3 %second_step_kernel.1 = bf16[8,16,16,128]{3,2,1,0:T(8,128)(2,1)S(1)} custom-call(f32[8,20,16,128]{3,2,1,0:T(8,128)S(1)} %get-tuple-element.17.x_ref, f32[8,16,16,128]{3,2,1,0:T(8,128)S(1)} %get-tuple-element.18.d_ref, f32[128,128]{1,0:T(8,128)S(1)} %bitcast.21, bf16[2304,256]{1,0:T(8,128)(2,1)S(1)} %get-tuple-element.15.w1_ref, f32[1,256]{1,0:T(1,128)S(1)} %bitcast.24, ...), custom_call_target="tpu_custom_call" | custom-call | tf_op jit(solution)/shard_map/second_step_kernel/pallas_call | solution.py:22
  92.9 0.0 copy-start.3
  92.9 14.5 %all_to_all.21 = bf16[8,16,16,128]{3,2,1,0:T(8,128)(2,1)S(1)} all-to-all(bf16[8,16,16,128]{3,2,1,0:T(8,128)(2,1)S(1)} %second_step_kernel.1), channel_id=1, replica_groups=mesh['traj_0'=4,'traj_1'=2,'lon_0'=2,'lon_1'=4,'lon_2'=2] {'traj_0','tra..., dimensions={0} | all-to-all | bytes 1048576 | tf_op jit(solution)/shard_map/all_to_all | solution.py:309
  107.4 0.0 copy-done.3
  107.4 1.6 %finish_kernel.1 = f32[1248,128]{1,0:T(8,128)} custom-call(bf16[128,16,128]{2,1,0:T(8,128)(2,1)S(1)} %bitcast.16, f32[128,16,128]{2,1,0:T(8,128)S(1)} %copy-done.3), custom_call_target="tpu_custom_call" | custom-call | tf_op jit(solution)/shard_map/finish_kernel/pallas_call | solution.py:22
  (1 shorter events, 0.0 us)
Async XLA Ops:
  1.0 1.1 copy-start.4
  2.1 0.7 copy-start.6
  5.9 1.0 copy-start.2
  6.9 20.8 %all-to-all-start.1 = ((f32[128,1,128]{2,1,0:T(1,128)}), f32[128,1,128]{2,1,0:T(1,128)S(1)}, u32[]{:S(2)}, u32[]{:S(2)}) async-start(f32[128,1,128]{2,1,0:T(1,128)} %bitcast.4), calls=%async_computation.1 | async-start | bytes 131072 | tf_op jit(solution)/shard_map/all_to_all | solution.py:240
  18.1 4.5 %collective-permute-start.1 = (bf16[4,32,128]{2,1,0:T(8,128)(2,1)S(1)}, bf16[4,32,128]{2,1,0:T(8,128)(2,1)S(1)}, u32[]{:S(2)}, u32[]{:S(2)}) collective-permute-start(bf16[4,32,128]{2,1,0:T(8,128)(2,1)S(1)} %get-tuple-element.21), channel_id=1, source_target_pairs={{1,0},{2,1},{3,2},{4,3},{5,4},{6,5},{7,6},{8,7},{9,8},{10,9},{11,1... | collective-permute-start | bytes 98312 | tf_op jit(solution)/shard_map/ppermute | solution.py:270
  20.9 5.4 %collective-permute-start = (bf16[4,32,128]{2,1,0:T(8,128)(2,1)S(1)}, bf16[4,32,128]{2,1,0:T(8,128)(2,1)S(1)}, u32[]{:S(2)}, u32[]{:S(2)}) collective-permute-start(bf16[4,32,128]{2,1,0:T(8,128)(2,1)S(1)} %get-tuple-element.22), channel_id=1, source_target_pairs={{0,1},{1,2},{2,3},{3,4},{4,5},{5,6},{6,7},{7,8},{8,9},{9,10},{10,1... | collective-permute-start | bytes 98312 | tf_op jit(solution)/shard_map/ppermute | solution.py:269
  27.7 7.1 %copy-start = (bf16[234,2304]{1,0:T(8,128)(2,1)S(1)}, bf16[234,2304]{1,0:T(8,128)(2,1)}, u32[]{:S(2)}) copy-start(bf16[234,2304]{1,0:T(8,128)(2,1)} %w2_ref.1) | copy-start | bytes 3234820
  27.7 26.9 %all-to-all-start = ((bf16[8,24,32,128]{3,2,1,0:T(8,128)(2,1)}), bf16[8,24,32,128]{3,2,1,0:T(8,128)(2,1)}, u32[]{:S(2)}, u32[]{:S(2)}) async-start(bf16[8,24,32,128]{3,2,1,0:T(8,128)(2,1)} %assemble_kernel.1), calls=%async_computation | async-start | bytes 3145728 | tf_op jit(solution)/shard_map/all_to_all | solution.py:287
  34.8 19.8 %copy-start.5 = (f32[256]{0:T(256)S(1)}, f32[256]{0:T(256)}, u32[]{:S(2)}) copy-start(f32[256]{0:T(256)} %param.10) | copy-start | bytes 3076
  34.8 1.2 %copy-start.1 = (bf16[256,2106]{0,1:T(8,128)(2,1)S(1)}, bf16[256,2106]{0,1:T(8,128)(2,1)}, u32[]{:S(2)}) copy-start(bf16[256,2106]{0,1:T(8,128)(2,1)} %param.9) | copy-start | bytes 3234820
  92.9 14.5 %copy-start.3 = (f32[128,16,128]{2,1,0:T(8,128)S(1)}, f32[128,16,128]{2,1,0:T(8,128)}, u32[]{:S(2)}) copy-start(f32[128,16,128]{2,1,0:T(8,128)} %copy-done.2) | copy-start | bytes 3145732
where the time goes:
time: 109 us
  Pallas kernels  30.8 us (28%)
  blocking collectives  29 us (27%)
  waiting for transfers between devices  22.9 us (21%)
  starting transfers between devices  21.2 us (19%)
  local copies, waits for them, and re-layouts  5 us (5%)
    pallas_call x6, Pallas kernels, call(): pl.pallas_call(kernel, out_shape=outs, in_specs=[VMEM] * len(args), out_s...  30.8 us
    all_to_all x1, waiting for transfers between devices, body(): got = lax.all_to_all(sent, TRAJ, 0, 0)  17.5 us
    all_to_all x1, blocking collectives, body(): back = lax.all_to_all(d2, TRAJ, 0, 0)  14.5 us
    all_to_all x1, blocking collectives, exchanged(): return lax.all_to_all(rows[:, None, :], axes, 0, 0)[:, 0, :]  14.5 us
    all_to_all x1, starting transfers between devices, exchanged(): return lax.all_to_all(rows[:, None, :], axes, 0, 0)[:, 0, :]  11.2 us
    all_to_all x1, starting transfers between devices, body(): got = lax.all_to_all(sent, TRAJ, 0, 0)  7.13 us
    unnamed x15, local copies, waits for them, and re-layouts  5 us
    ppermute x1, waiting for transfers between devices, body(): left = lax.ppermute(packed[cols - wide:], LON, up)  3.85 us
  transfers between devices with their start and end apart: 4, of which 3 were waited for; matrix products, arithmetic and copies ran while one was open for 0% of the time, Pallas kernels for 2%

commit v1 on v0

--- a/solution.py
+++ b/solution.py
@@ -18,14 +18,14 @@
 VMEM = pl.BlockSpec(memory_space=pltpu.VMEM)
 
 
-def call(kernel, outs, scratch, *args):
+def call(kernel, outs, scratch, *args, far=0):
     return pl.pallas_call(
         kernel,
         out_shape=outs,
-        in_specs=[VMEM] * len(args),
+        in_specs=[pl.BlockSpec(memory_space=pltpu.HBM)] * far + [VMEM] * (len(args) - far),
         out_specs=[VMEM] * len(outs),
         scratch_shapes=scratch,
-        compiler_params=pltpu.CompilerParams(vmem_limit_bytes=48 * 2**20),
+        compiler_params=pltpu.CompilerParams(vmem_limit_bytes=16 * 2**20),
         name=kernel.func.__name__ if isinstance(kernel, functools.partial) else kernel.__name__,
     )(*args)
 
@@ -34,51 +34,76 @@
     return lax.broadcasted_iota(jnp.int32, shape, dim)
 
 
-def prepare_kernel(nvar, x_ref, index_ref, values_ref, send_ref, base_ref, sums_ref, xs, xf, vs):
-    lines, cols = x_ref.shape
-    rows = lines // nvar
-    xs[...] = jnp.zeros_like(xs)
-    xs[:lines, :] = x_ref[...]
+def fetch(nvar, x_ref, index_ref, values_ref, xs, xf, vs, index, values, sems):
+    copies = [
+        pltpu.make_async_copy(x_ref, xs.at[: x_ref.shape[0]], sems.at[0]),
+        pltpu.make_async_copy(index_ref, index, sems.at[1]),
+        pltpu.make_async_copy(values_ref, values, sems.at[2]),
+    ]
+    for copy in copies:
+        copy.start()
+    cols = xs.shape[1]
+    rows = xf.shape[0] // cols
     vpad = xs.shape[0] // rows
-    for r in range(rows):
-        picked = xs[pl.ds(r, vpad, stride=rows), :]
-        picked = jnp.concatenate([picked, jnp.zeros((LANES - vpad, cols), F32)], 0)
-        xf[pl.ds(r, cols, stride=rows), :] = picked.T
+    xs[nvar * rows :, :] = jnp.zeros((xs.shape[0] - nvar * rows, cols), F32)
     vs[...] = jnp.zeros_like(vs)
-    vs[:, :nvar] = values_ref[...]
-    turned = vs[...]
+    for copy in copies:
+        copy.wait()
+    vs[:nvar, :] = values[:, 0, :]
+    turned = vs[...].T
     high = turned.astype(BF16)
     rest = turned - high.astype(F32)
     middle = rest.astype(BF16)
     low = (rest - middle.astype(F32)).astype(BF16)
     table = jnp.concatenate([high, middle, low, jnp.ones_like(high)], 1)
-    index = index_ref[...]
-    place = (index % LANES) * rows + index // (16 * LANES)
-    chunk = 256
-    nobs = index.shape[1]
-
-    def one(i, acc):
-        at = pl.ds(i * chunk, chunk)
-        x = xf[at, :]
-        cell = iota((chunk, nobs), 0) + i * chunk
+    place = (index[...] % LANES) * rows + index[...] // (16 * LANES)
+    for r in range(rows):
+        picked = xs[pl.ds(r, vpad, stride=rows), :]
+        picked = jnp.concatenate([picked, jnp.zeros((LANES - vpad, cols), F32)], 0)
+        xf[pl.ds(r, cols, stride=rows), :] = picked.T
+
+    def observed(start, size):
+        cell = iota((size, index.shape[1]), 0) + start
         picks = jnp.where(cell == place, 1.0, 0.0).astype(BF16)
         found = jnp.dot(picks, table, preferred_element_type=F32)
         obs = (found[:, :LANES] + found[:, LANES : 2 * LANES]) + found[:, 2 * LANES : 3 * LANES]
-        keep = 1.0 - 0.5 * found[:, 3 * LANES :]
-        lane = iota((chunk, LANES), 1)
+        return obs, 1.0 - 0.5 * found[:, 3 * LANES :]
+
+    return observed
+
+
+CHUNK = 256
+
+
+def prepare_kernel(nvar, x_ref, index_ref, values_ref, send_ref, sums_ref, xs, xf, *rest):
+    observed = fetch(nvar, x_ref, index_ref, values_ref, xs, xf, *rest)
+    rows = send_ref.shape[1] // 2
+    each = CHUNK // rows
+    acc = jnp.zeros((8, LANES), F32)
+    for i in range(xf.shape[0] // CHUNK):
+        x = xf[i * CHUNK : (i + 1) * CHUNK, :]
+        obs, keep = observed(i * CHUNK, CHUNK)
+        lane = iota(x.shape, 1)
         coarse = x.astype(BF16).astype(F32)
         fine = pltpu.roll(x - coarse, nvar, 1)
         again = pltpu.roll(fine, nvar, 1)
         state = jnp.where(lane < nvar, coarse, fine)
         seen = jnp.where(lane < nvar, obs, jnp.where(lane == LANES - 1, keep, again))
-        out = pl.ds(i * (chunk // rows), chunk // rows)
-        send_ref[out, :rows] = state.astype(BF16).reshape(chunk // rows, rows, LANES)
-        send_ref[out, rows:] = seen.astype(BF16).reshape(chunk // rows, rows, LANES)
-        base_ref[out] = (keep * keep * x + (keep + 1.0) * 0.5 * obs).reshape(chunk // rows, rows, LANES)
-        return acc + jnp.sum((x * x).reshape(chunk // 8, 8, LANES), 0)
-
-    acc = lax.fori_loop(0, cols * rows // chunk, one, jnp.zeros((8, LANES), F32))
+        send_ref[i * each : (i + 1) * each, :rows] = state.astype(BF16).reshape(each, rows, LANES)
+        send_ref[i * each : (i + 1) * each, rows:] = seen.astype(BF16).reshape(each, rows, LANES)
+        acc = acc + jnp.sum((x * x).reshape(CHUNK // 8, 8, LANES), 0)
     sums_ref[...] = jnp.broadcast_to(jnp.sum(acc, 0, keepdims=True), sums_ref.shape)
+
+
+def base_kernel(nvar, x_ref, index_ref, values_ref, after_ref, base_ref, xs, xf, *rest):
+    observed = fetch(nvar, x_ref, index_ref, values_ref, xs, xf, *rest)
+    rows = base_ref.shape[1]
+    each = CHUNK // rows
+    for i in range(xf.shape[0] // CHUNK):
+        x = xf[i * CHUNK : (i + 1) * CHUNK, :]
+        obs, keep = observed(i * CHUNK, CHUNK)
+        base = keep * keep * x + (keep + 1.0) * 0.5 * obs
+        base_ref[i * each : (i + 1) * each] = base.reshape(each, rows, LANES)
 
 
 def weights_kernel(nvar, w1_ref, w2_ref, w1t_ref, w2t_ref, pad, flat):
@@ -104,18 +129,33 @@
             w2t_ref[pl.ds((3 * d + b) * hid, hid), :] = block.astype(BF16)
 
 
-def assemble_kernel(reach, x_ref, left_ref, right_ref, out_ref):
+def assemble_kernel(reach, x_ref, left_ref, right_ref, moments_ref, out_ref, done_ref):
     parts = out_ref.shape[0]
     cols = x_ref.shape[0]
+    rows = x_ref.shape[1] // 2
     each = cols // parts
-    for k in range(parts):
+    total = jnp.broadcast_to(jnp.sum(moments_ref[...], 0, keepdims=True), (rows, LANES))
+    high = total.astype(BF16).astype(F32)
+    middle = (total - high).astype(BF16).astype(F32)
+    row = iota(total.shape, 0)
+    total = jnp.where(row == 0, high, jnp.where(row == 1, middle, jnp.where(row == 2, total - high - middle, 0.0)))
+    total = total.astype(BF16)
+
+    def fill(k, reach, half, to, skip):
         first, last = k * each - reach, (k + 1) * each + reach
         lo, hi = max(first, 0), min(last, cols)
-        out_ref[k, lo - first : hi - first] = x_ref[lo:hi]
+        half = slice(half * rows, (half + 1) * rows)
+        out_ref[k, to + lo - first : to + hi - first] = x_ref[lo:hi, half]
         if first < 0:
-            out_ref[k, :-first] = left_ref[...]
+            out_ref[k, to : to - first] = left_ref[skip:, half]
         if last > cols:
-            out_ref[k, hi - first :] = right_ref[...]
+            out_ref[k, to + hi - first : to + last - first] = right_ref[:reach, half]
+
+    for k in range(parts):
+        fill(k, reach, 0, 0, 0)
+        fill(k, reach // 2, 1, each + 2 * reach, reach - reach // 2)
+        out_ref[k, 2 * each + 3 * reach] = total
+    done_ref[...] = moments_ref[:8, :]
 
 
 def moved(value, by, edge):
@@ -123,12 +163,13 @@
     return jnp.where(row == edge, 0.0, pltpu.roll(value, by % value.shape[0], 0))
 
 
-def convolutions(nvar, read, parts_ref, w1_ref, bias_ref, w2_ref, window, hidden, count, write):
+def convolutions(nvar, read, total, w2_far, w1_ref, bias_ref, window, hidden, w2_ref, sem, count, write):
+    copy = pltpu.make_async_copy(w2_far, w2_ref, sem)
+    copy.start()
     states, cols = window.shape[0] - 2, window.shape[1]
     rows = window.shape[2]
     inner = hidden.shape[1]
     outer = inner - 2
-    total = jnp.sum(parts_ref[...], 0, keepdims=True)
     scale = 1.0 / jnp.sqrt(total / count + 1e-06)
     for edge in (0, states + 1):
         window[edge] = jnp.zeros(window.shape[1:], BF16)
@@ -144,8 +185,6 @@
         window[t + 1] = jnp.concatenate([low, high], 1).astype(BF16).reshape(cols, rows, 2 * LANES)
         return 0
 
-    lax.fori_loop(0, states, fill, 0)
-
     def first(t, _):
         patches = [
             window[t + d, b : b + inner].reshape(inner * rows, 2 * LANES) for d in range(3) for b in range(3)
@@ -155,8 +194,6 @@
         value = value * (1.0 + jnp.tanh(value))
         hidden[t + 1] = value.astype(BF16).reshape(inner, rows, value.shape[1])
         return 0
-
-    lax.fori_loop(0, states, first, 0)
 
     def second(t, carry):
         patches = [
@@ -170,11 +207,21 @@
         score = moved(low, 1, 0) + mid + moved(end, -1, 15)
         return write(t, jnp.where(lane < nvar, score, 0.0), carry)
 
-    return lax.fori_loop(0, states, second, jnp.zeros((8, LANES), F32))
-
-
-def first_step_kernel(nvar, count, s_ref, parts_ref, w1_ref, bias_ref, w2_ref, x_ref, d_ref, sums_ref, window, hidden):
-    rows = s_ref.shape[2] // 2
+    carry = jnp.zeros((8, LANES), F32)
+    for t in range(states + 2):
+        if t < states:
+            fill(t, 0)
+        if 1 <= t <= states:
+            first(t - 1, 0)
+        if t == 2:
+            copy.wait()
+        if t >= 2:
+            carry = second(t - 2, carry)
+    return carry
+
+
+def first_step_kernel(nvar, count, w2_ref, s_ref, w1_ref, bias_ref, x_ref, d_ref, sums_ref, window, hidden, w2, sem):
+    rows = s_ref.shape[2]
     wide = window.shape[1]
     outer = x_ref.shape[1]
     core = d_ref.shape[1]
@@ -182,19 +229,21 @@
     ring = (wide - outer) // 2
 
     def read(t):
-        state = s_ref[t, :, :rows].astype(F32).reshape(wide * rows, LANES)
-        seen = s_ref[t, :, rows:].astype(F32).reshape(wide * rows, LANES)
+        state = s_ref[t, :wide].astype(F32).reshape(wide * rows, LANES)
+        seen = s_ref[t, wide : wide + outer].astype(F32).reshape(outer * rows, LANES)
         lane = iota(state.shape, 1)
         left = LANES - nvar
-        fine = jnp.where(lane < left, pltpu.roll(state, left, 1), pltpu.roll(seen, 2 * left, 1))
+        none = jnp.zeros((ring * rows, LANES), F32)
+        rest = jnp.concatenate([none, pltpu.roll(seen, 2 * left, 1), none], 0)
+        fine = jnp.where(lane < left, pltpu.roll(state, left, 1), rest)
         x = jnp.where(lane < nvar, state + fine, 0.0)
-        mixed = (seen[:, LANES - 1 :] * x + 0.5 * seen).reshape(wide, rows, LANES)
-        x_ref[t] = mixed[ring : ring + outer]
+        mixed = seen[:, LANES - 1 :] * x[ring * rows : (ring + outer) * rows] + 0.5 * seen
+        x_ref[t] = mixed.reshape(outer, rows, LANES)
         return x
 
     def write(t, score, acc):
         mixed = x_ref[t].reshape(outer * rows, LANES)
-        keep = s_ref[t, ring : ring + outer, rows:].astype(F32).reshape(outer * rows, LANES)[:, LANES - 1 :]
+        keep = s_ref[t, wide : wide + outer].astype(F32).reshape(outer * rows, LANES)[:, LANES - 1 :]
         half = 0.5 * score
         lane = iota(score.shape, 1)
         x = jnp.where(lane < nvar, mixed + half, 0.0)
@@ -203,11 +252,12 @@
         own = x.reshape(outer, rows, LANES)[skip : skip + core]
         return acc + jnp.sum((own * own).reshape(core * rows // 8, 8, LANES), 0)
 
-    acc = convolutions(nvar, read, parts_ref, w1_ref, bias_ref, w2_ref, window, hidden, count, write)
+    total = jnp.sum(s_ref[:, wide + outer].astype(F32).reshape(-1, LANES), 0, keepdims=True)
+    acc = convolutions(nvar, read, total, w2_ref, w1_ref, bias_ref, window, hidden, w2, sem, count, write)
     sums_ref[...] = jnp.broadcast_to(jnp.sum(acc, 0, keepdims=True), sums_ref.shape)
 
 
-def second_step_kernel(nvar, count, x_ref, d_ref, parts_ref, w1_ref, bias_ref, w2_ref, out_ref, window, hidden):
+def second_step_kernel(nvar, count, w2_ref, x_ref, d_ref, parts_ref, w1_ref, bias_ref, out_ref, window, hidden, w2, sem):
     wide, rows = x_ref.shape[1], x_ref.shape[2]
     core = d_ref.shape[1]
 
@@ -222,7 +272,8 @@
         out_ref[t] = d.astype(BF16).reshape(core, rows, LANES)
         return acc
 
-    convolutions(nvar, read, parts_ref, w1_ref, bias_ref, w2_ref, window, hidden, count, write)
+    total = jnp.sum(parts_ref[...], 0, keepdims=True)
+    convolutions(nvar, read, total, w2_ref, w1_ref, bias_ref, window, hidden, w2, sem, count, write)
 
 
 def finish_kernel(nvar, d_ref, base_ref, out_ref, both):
@@ -251,17 +302,22 @@
     sds = jax.ShapeDtypeStruct
     everyone = sds((parts * bands, LANES), F32)
     band = (cols, rows, LANES)
-    packed, base, sums = call(
+    source = (states.reshape(nvar * rows, cols), obs_index, obs_values.transpose(1, 0, 2))
+    source = [pltpu.with_memory_space_constraint(value, pltpu.HBM) for value in source]
+    scratch = [
+        pltpu.VMEM((vpad * rows, cols), F32),
+        pltpu.VMEM((cols * rows, LANES), F32),
+        pltpu.VMEM((LANES, obs_index.shape[1]), F32),
+        pltpu.VMEM(obs_index.shape, jnp.int32),
+        pltpu.VMEM((nvar, 1, obs_index.shape[1]), F32),
+        pltpu.SemaphoreType.DMA((3,)),
+    ]
+    packed, sums = call(
         functools.partial(prepare_kernel, nvar),
-        [sds((cols, 2 * rows, LANES), BF16), sds(band, F32), everyone],
-        [
-            pltpu.VMEM((vpad * rows, cols), F32),
-            pltpu.VMEM((cols * rows, LANES), F32),
-            pltpu.VMEM((obs_index.shape[1], LANES), F32),
-        ],
-        states.reshape(nvar * rows, cols),
-        obs_index,
-        obs_values[0].T,
+        [sds((cols, 2 * rows, LANES), BF16), sds((bands, LANES), F32)],
+        scratch,
+        *source,
+        far=3,
     )
     wide = 2 * STEPS
     up = [(i, (i + 1) % bands) for i in range(bands)]
@@ -276,35 +332,48 @@
         second_weight,
     )
     bias = first_bias[None]
-    (sent,) = call(
+    sent, done = call(
         functools.partial(assemble_kernel, wide),
-        [sds((parts, each + 2 * wide, 2 * rows, LANES), BF16)],
+        [sds((parts, 2 * each + 3 * wide + 1, rows, LANES), BF16), sds((8, LANES), F32)],
         [],
         packed,
         left,
         right,
+        exchanged(sums, LON),
     )
     got = lax.all_to_all(sent, TRAJ, 0, 0)
+    (base,) = call(functools.partial(base_kernel, nvar), [sds(band, F32)], scratch, *source, done, far=4)
+    w2 = pltpu.with_memory_space_constraint(w2, pltpu.HBM)
+
+    def buffers(cols):
+        return [
+            pltpu.VMEM((parts + 2, cols, rows, hid), BF16),
+            pltpu.VMEM((parts + 2, cols - 2, rows, hid), BF16),
+            pltpu.VMEM(w2.shape, BF16),
+            pltpu.SemaphoreType.DMA(()),
+        ]
+
     x1, d1, sums1 = call(
         functools.partial(first_step_kernel, nvar, count),
         [sds((parts, each + 4, rows, LANES), F32), sds((parts, each, rows, LANES), F32), everyone],
-        [pltpu.VMEM((parts + 2, each + 8, rows, hid), BF16), pltpu.VMEM((parts + 2, each + 6, rows, hid), BF16)],
+        buffers(each + 8),
+        w2,
         got,
-        exchanged(sums, ALL),
         w1,
         bias,
-        w2,
+        far=1,
     )
     (d2,) = call(
         functools.partial(second_step_kernel, nvar, count),
         [sds((parts, each, rows, LANES), BF16)],
-        [pltpu.VMEM((parts + 2, each + 4, rows, hid), BF16), pltpu.VMEM((parts + 2, each + 2, rows, hid), BF16)],
+        buffers(each + 4),
+        w2,
         x1,
         d1,
         exchanged(sums1, ALL),
         w1,
         bias,
-        w2,
+        far=1,
     )
     back = lax.all_to_all(d2, TRAJ, 0, 0)
     (out,) = call(

time: 109 us -> 91.9 us (0.84)
  Pallas kernels: 30.8 us -> 23.5 us
  blocking collectives: 29 us -> 22.6 us
  starting transfers between devices: 21.2 us -> 15.1 us
  waiting for transfers between devices: 22.9 us -> 26.7 us
  local copies, waits for them, and re-layouts: 5 us -> 3.53 us
    all_to_all x1 -> x0, blocking collectives: 14.5 us -> none  [body(): back = lax.all_to_all(d2, TRAJ, 0, 0)]
    all_to_all x1, waiting for transfers between devices: 0.01 us -> 9.5 us  [body(): back = lax.all_to_all(d2, TRAJ, 0, 0)]
    all_to_all x1 -> x2, blocking collectives: 14.5 us -> 22.6 us  [exchanged(): return lax.all_to_all(rows[:, None, :], axes, 0, 0)[:, 0, :]]
    all_to_all x1, starting transfers between devices: 11.2 us -> 3.51 us  [body(): back = lax.all_to_all(d2, TRAJ, 0, 0)]
    pallas_call x6 -> x7, Pallas kernels: 30.8 us -> 23.5 us  [call(): pl.pallas_call(kernel, out_shape=outs, in_specs=[pl.BlockSpec(memory_spac...]
    ppermute x1, waiting for transfers between devices: 3.85 us -> 0.01 us  [body(): left = lax.ppermute(packed[cols - wide:], LON, up)]
    ppermute x1, waiting for transfers between devices: 1.59 us -> 0.01 us  [body(): right = lax.ppermute(packed[:wide], LON, down)]
    unnamed x15 -> x8, local copies, waits for them, and re-layouts: 5 us -> 3.52 us
  transfers between devices with their start and end apart: 4 -> 4, of which waited for: 3 -> 2; matrix products, arithmetic and copies ran while one was open for 0% -> 0% of each run, Pallas kernels for 2% -> 4%
where the time goes in v1:
time: 91.9 us; the launch traced here: 91.5 us
  waiting for transfers between devices  26.7 us (29%)
  Pallas kernels  23.5 us (26%)
  blocking collectives  22.6 us (25%)
  starting transfers between devices  15.1 us (16%)
  local copies, waits for them, and re-layouts  3.53 us (4%)
    pallas_call x7, Pallas kernels, call(): pl.pallas_call(kernel, out_shape=outs, in_specs=[pl.BlockSpec(memory_spac...  23.5 us
    all_to_all x2, blocking collectives, exchanged(): return lax.all_to_all(rows[:, None, :], axes, 0, 0)[:, 0, :]  22.6 us
    all_to_all x1, waiting for transfers between devices, body(): got = lax.all_to_all(sent, TRAJ, 0, 0)  17.2 us
    all_to_all x1, waiting for transfers between devices, body(): back = lax.all_to_all(d2, TRAJ, 0, 0)  9.5 us
    all_to_all x1, starting transfers between devices, body(): got = lax.all_to_all(sent, TRAJ, 0, 0)  7.64 us
    ppermute x1, starting transfers between devices, body(): right = lax.ppermute(packed[:wide], LON, down)  3.84 us
    unnamed x8, local copies, waits for them, and re-layouts  3.52 us
    all_to_all x1, starting transfers between devices, body(): back = lax.all_to_all(d2, TRAJ, 0, 0)  3.51 us
  transfers between devices with their start and end apart: 4, of which 2 were waited for; matrix products, arithmetic and copies ran while one was open for 0% of the time, Pallas kernels for 4%

profile of v1, /device:TPU:0, one launch (start us, length us, event | category | flops | bytes accessed | tf_op | source)
XLA Modules:
  0.0 91.5 jit_solution(11332631533012319884)
XLA Ops:
  0.0 2.6 %prepare_kernel.1 = (bf16[128,32,128]{2,1,0:T(8,128)(2,1)S(1)}, f32[16,128]{1,0:T(8,128)S(1)}) custom-call(f32[1248,128]{1,0:T(8,128)} %bitcast.22, s32[1,256]{1,0:T(1,128)} %index_ref.3, f32[78,1,256]{2,1,0:T(1,128)} %bitcast.24), custom_call_target="tpu_custom_call" | custom-call | tf_op jit(solution)/shard_map/prepare_kernel/pallas_call | solution.py:22
  2.6 0.1 collective-permute-start
  2.7 3.8 %collective-permute-start.1 = (bf16[4,32,128]{2,1,0:T(8,128)(2,1)S(1)}, bf16[4,32,128]{2,1,0:T(8,128)(2,1)S(1)}, u32[]{:S(2)}, u32[]{:S(2)}) collective-permute-start(bf16[4,32,128]{2,1,0:T(8,128)(2,1)S(1)} %get-tuple-element.23), channel_id=1, source_target_pairs={{1,0},{2,1},{3,2},{4,3},{5,4},{6,5},{7,6},{8,7},{9,8},{10,9},{11,1... | collective-permute-start | bytes 98312 | tf_op jit(solution)/shard_map/ppermute | solution.py:326
  6.5 9.3 %all_to_all.20 = f32[16,1,128]{2,1,0:T(1,128)S(1)} all-to-all(f32[16,1,128]{2,1,0:T(1,128)S(1)} %bitcast.19), channel_id=1, replica_groups=mesh['traj_0'=4,'traj_1'=2,'lon_0'=2,'lon_1'=4,'lon_2'=2] {'lon_0','lon_..., dimensions={0} | all-to-all | bytes 16384 | tf_op jit(solution)/shard_map/all_to_all | solution.py:291
  15.8 0.0 collective-permute-done.left_ref
  15.8 0.0 collective-permute-done.1.right_ref
  15.8 1.3 %assemble_kernel.1 = (bf16[8,45,16,128]{3,2,1,0:T(8,128)(2,1)}, f32[8,128]{1,0:T(8,128)S(1)}) custom-call(bf16[128,32,128]{2,1,0:T(8,128)(2,1)S(1)} %get-tuple-element.15.x_ref, bf16[4,32,128]{2,1,0:T(8,128)(2,1)S(1)} %collective-permute-done.left_ref, bf16[4,32,128]{2,1,0:T(8,128)(2,1)S(1)} %collective-permute-done.1.right_ref, f32[16,128]{1,0:T(8,128)S(1)} %bitcast.18), custom_call_target="tpu_custom_call" | custom-call | tf_op jit(solution)/shard_map/assemble_kernel/pallas_call | solution.py:22
  17.1 7.6 %all-to-all-start.1 = ((bf16[8,45,16,128]{3,2,1,0:T(8,128)(2,1)}), bf16[8,45,16,128]{3,2,1,0:T(8,128)(2,1)S(1)}, u32[]{:S(2)}, u32[]{:S(2)}) async-start(bf16[8,45,16,128]{3,2,1,0:T(8,128)(2,1)} %get-tuple-element.17), calls=%async_computation.1 | async-start | bytes 2949120 | tf_op jit(solution)/shard_map/all_to_all | solution.py:344
  24.7 0.0 copy-start.3
  24.7 0.0 copy-start.1
  24.7 1.2 %copy-done.1 = bf16[234,2304]{1,0:T(8,128)(2,1)S(1)} copy-done((bf16[234,2304]{1,0:T(8,128)(2,1)S(1)}, bf16[234,2304]{1,0:T(8,128)(2,1)}, u32[]{:S(2)}) %copy-start.1) | copy-done | bytes 1078296
  26.0 0.0 copy-start.2
  26.0 1.2 %copy-done.2 = bf16[256,2106]{0,1:T(8,128)(2,1)S(1)} copy-done((bf16[256,2106]{0,1:T(8,128)(2,1)S(1)}, bf16[256,2106]{0,1:T(8,128)(2,1)}, u32[]{:S(2)}) %copy-start.2) | copy-done | bytes 1078296
  27.2 1.1 %weights_kernel.1 = (bf16[2304,256]{1,0:T(8,128)(2,1)S(1)}, bf16[2304,256]{1,0:T(8,128)(2,1)S(1)}) custom-call(bf16[2106,256]{1,0:T(8,128)(2,1)S(1)} %bitcast.15, bf16[234,2304]{1,0:T(8,128)(2,1)S(1)} %copy-done.1), custom_call_target="tpu_custom_call" | custom-call | tf_op jit(solution)/shard_map/weights_kernel/pallas_call | solution.py:22
  28.3 0.0 copy-start
  28.3 1.0 %copy-done = bf16[2304,256]{1,0:T(8,128)(2,1)} copy-done((bf16[2304,256]{1,0:T(8,128)(2,1)}, bf16[2304,256]{1,0:T(8,128)(2,1)S(1)}, u32[]{:S(2)}) %copy-start) | copy-done | bytes 1179672
  29.4 17.2 %all-to-all-done.1.s_ref = bf16[8,45,16,128]{3,2,1,0:T(8,128)(2,1)S(1)} async-done(((bf16[8,45,16,128]{3,2,1,0:T(8,128)(2,1)}), bf16[8,45,16,128]{3,2,1,0:T(8,128)(2,1)S(1)}, u32[]{:S(2)}, u32[]{:S(2)}) %all-to-all-start.1) | async-done | bytes 1474592 | tf_op jit(solution)/shard_map/all_to_all | solution.py:344
  46.5 0.0 copy-done.3
  46.6 7.5 %first_step_kernel.1 = (f32[8,20,16,128]{3,2,1,0:T(8,128)S(1)}, f32[8,16,16,128]{3,2,1,0:T(8,128)S(1)}, f32[128,128]{1,0:T(8,128)S(1)}) custom-call(bf16[2304,256]{1,0:T(8,128)(2,1)} %copy-done, bf16[8,45,16,128]{3,2,1,0:T(8,128)(2,1)S(1)} %all-to-all-done.1.s_ref, bf16[2304,256]{1,0:T(8,128)(2,1)S(1)} %get-tuple-element.18.w1_ref, f32[1,256]{1,0:T(1,128)S(1)} %bitcast.20), custom_call_target="tpu_custom_call" | custom-call | tf_op jit(solution)/shard_map/first_step_kernel/pallas_call | solution.py:22
  54.1 13.3 %all_to_all.21 = f32[128,1,128]{2,1,0:T(1,128)S(1)} all-to-all(f32[128,1,128]{2,1,0:T(1,128)S(1)} %bitcast.17), channel_id=1, replica_groups=mesh['traj_0'=4,'traj_1'=2,'lon_0'=2,'lon_1'=4,'lon_2'=2] {'traj_0','tra..., dimensions={0} | all-to-all | bytes 131072 | tf_op jit(solution)/shard_map/all_to_all | solution.py:291
  67.4 7.3 %second_step_kernel.1 = bf16[8,16,16,128]{3,2,1,0:T(8,128)(2,1)} custom-call(bf16[2304,256]{1,0:T(8,128)(2,1)} %copy-done, f32[8,20,16,128]{3,2,1,0:T(8,128)S(1)} %get-tuple-element.19.x_ref, f32[8,16,16,128]{3,2,1,0:T(8,128)S(1)} %get-tuple-element.20.d_ref, f32[128,128]{1,0:T(8,128)S(1)} %bitcast.16, bf16[2304,256]{1,0:T(8,128)(2,1)S(1)} %get-tuple-element.18.w1_ref, ...), custom_call_target="tpu_custom_call" | custom-call | tf_op jit(solution)/shard_map/second_step_kernel/pallas_call | solution.py:22
  74.7 3.5 %all-to-all-start.3 = ((bf16[8,16,16,128]{3,2,1,0:T(8,128)(2,1)}), bf16[8,16,16,128]{3,2,1,0:T(8,128)(2,1)S(1)}, u32[]{:S(2)}, u32[]{:S(2)}) async-start(bf16[8,16,16,128]{3,2,1,0:T(8,128)(2,1)} %second_step_kernel.1), calls=%async_computation.3 | async-start | bytes 1048576 | tf_op jit(solution)/shard_map/all_to_all | solution.py:378
  78.2 2.2 %base_kernel.1.base_ref = f32[128,16,128]{2,1,0:T(8,128)S(1)} custom-call(f32[1248,128]{1,0:T(8,128)} %bitcast.23, s32[1,256]{1,0:T(1,128)} %index_ref.3, f32[78,1,256]{2,1,0:T(1,128)} %bitcast.25, f32[8,128]{1,0:T(8,128)S(1)} %get-tuple-element.22.after_ref), custom_call_target="tpu_custom_call" | custom-call | tf_op jit(solution)/shard_map/base_kernel/pallas_call | solution.py:22
  80.4 9.5 %all-to-all-done.3 = bf16[8,16,16,128]{3,2,1,0:T(8,128)(2,1)S(1)} async-done(((bf16[8,16,16,128]{3,2,1,0:T(8,128)(2,1)}), bf16[8,16,16,128]{3,2,1,0:T(8,128)(2,1)S(1)}, u32[]{:S(2)}, u32[]{:S(2)}) %all-to-all-start.3) | async-done | bytes 524320 | tf_op jit(solution)/shard_map/all_to_all | solution.py:378
  89.9 1.6 %finish_kernel.1 = f32[1248,128]{1,0:T(8,128)} custom-call(bf16[128,16,128]{2,1,0:T(8,128)(2,1)S(1)} %bitcast.14, f32[128,16,128]{2,1,0:T(8,128)S(1)} %base_kernel.1.base_ref), custom_call_target="tpu_custom_call" | custom-call | tf_op jit(solution)/shard_map/finish_kernel/pallas_call | solution.py:22
  (1 shorter events, 0.0 us)
Async XLA Ops:
  2.6 13.2 %collective-permute-start = (bf16[4,32,128]{2,1,0:T(8,128)(2,1)S(1)}, bf16[4,32,128]{2,1,0:T(8,128)(2,1)S(1)}, u32[]{:S(2)}, u32[]{:S(2)}) collective-permute-start(bf16[4,32,128]{2,1,0:T(8,128)(2,1)S(1)} %get-tuple-element.24), channel_id=1, source_target_pairs={{0,1},{1,2},{2,3},{3,4},{4,5},{5,6},{6,7},{7,8},{8,9},{9,10},{10,1... | collective-permute-start | bytes 98312 | tf_op jit(solution)/shard_map/ppermute | solution.py:325
  2.7 13.1 %collective-permute-start.1 = (bf16[4,32,128]{2,1,0:T(8,128)(2,1)S(1)}, bf16[4,32,128]{2,1,0:T(8,128)(2,1)S(1)}, u32[]{:S(2)}, u32[]{:S(2)}) collective-permute-start(bf16[4,32,128]{2,1,0:T(8,128)(2,1)S(1)} %get-tuple-element.23), channel_id=1, source_target_pairs={{1,0},{2,1},{3,2},{4,3},{5,4},{6,5},{7,6},{8,7},{9,8},{10,9},{11,1... | collective-permute-start | bytes 98312 | tf_op jit(solution)/shard_map/ppermute | solution.py:326
  17.1 29.5 %all-to-all-start.1 = ((bf16[8,45,16,128]{3,2,1,0:T(8,128)(2,1)}), bf16[8,45,16,128]{3,2,1,0:T(8,128)(2,1)S(1)}, u32[]{:S(2)}, u32[]{:S(2)}) async-start(bf16[8,45,16,128]{3,2,1,0:T(8,128)(2,1)} %get-tuple-element.17), calls=%async_computation.1 | async-start | bytes 2949120 | tf_op jit(solution)/shard_map/all_to_all | solution.py:344
  24.7 21.8 %copy-start.3 = (f32[256]{0:T(256)S(1)}, f32[256]{0:T(256)}, u32[]{:S(2)}) copy-start(f32[256]{0:T(256)} %param.10) | copy-start | bytes 3076
  24.7 1.3 %copy-start.1 = (bf16[234,2304]{1,0:T(8,128)(2,1)S(1)}, bf16[234,2304]{1,0:T(8,128)(2,1)}, u32[]{:S(2)}) copy-start(bf16[234,2304]{1,0:T(8,128)(2,1)} %w2_ref.1) | copy-start | bytes 3234820
  26.0 1.2 %copy-start.2 = (bf16[256,2106]{0,1:T(8,128)(2,1)S(1)}, bf16[256,2106]{0,1:T(8,128)(2,1)}, u32[]{:S(2)}) copy-start(bf16[256,2106]{0,1:T(8,128)(2,1)} %param.9) | copy-start | bytes 3234820
  28.3 1.0 %copy-start = (bf16[2304,256]{1,0:T(8,128)(2,1)}, bf16[2304,256]{1,0:T(8,128)(2,1)S(1)}, u32[]{:S(2)}) copy-start(bf16[2304,256]{1,0:T(8,128)(2,1)S(1)} %get-tuple-element.14.w2_ref) | copy-start | bytes 3538948
  74.7 15.2 %all-to-all-start.3 = ((bf16[8,16,16,128]{3,2,1,0:T(8,128)(2,1)}), bf16[8,16,16,128]{3,2,1,0:T(8,128)(2,1)S(1)}, u32[]{:S(2)}, u32[]{:S(2)}) async-start(bf16[8,16,16,128]{3,2,1,0:T(8,128)(2,1)} %second_step_kernel.1), calls=%async_computation.3 | async-start | bytes 1048576 | tf_op jit(solution)/shard_map/all_to_all | solution.py:378

commit v2 on v1

--- a/solution.py
+++ b/solution.py
@@ -106,7 +106,7 @@
         base_ref[i * each : (i + 1) * each] = base.reshape(each, rows, LANES)
 
 
-def weights_kernel(nvar, w1_ref, w2_ref, w1t_ref, w2t_ref, pad, flat):
+def weights_kernel(nvar, w1_ref, w2_ref, out_ref, pad, flat):
     hid = w1_ref.shape[1]
     win = 3 * nvar
     rest = jnp.zeros((hid, hid - win), F32)
@@ -117,7 +117,7 @@
             for a in range(3):
                 at = (3 * a + b) * win + d * nvar
                 pad[a * nvar : (a + 1) * nvar, :] = flat[at : at + nvar, :]
-            w1t_ref[pl.ds((3 * d + b) * hid, hid), :] = pad[...].astype(BF16)
+            out_ref[0, (3 * d + b) * hid : (3 * d + b + 1) * hid, :] = pad[...].astype(BF16)
     for b in range(3):
         turned = []
         for a in range(3):
@@ -126,7 +126,7 @@
         for d in range(3):
             parts = [t[:, (2 - d) * nvar : (3 - d) * nvar] for t in turned]
             block = jnp.concatenate(parts + [rest], 1)
-            w2t_ref[pl.ds((3 * d + b) * hid, hid), :] = block.astype(BF16)
+            out_ref[1, (3 * d + b) * hid : (3 * d + b + 1) * hid, :] = block.astype(BF16)
 
 
 def assemble_kernel(reach, x_ref, left_ref, right_ref, moments_ref, out_ref, done_ref):
@@ -163,9 +163,7 @@
     return jnp.where(row == edge, 0.0, pltpu.roll(value, by % value.shape[0], 0))
 
 
-def convolutions(nvar, read, total, w2_far, w1_ref, bias_ref, window, hidden, w2_ref, sem, count, write):
-    copy = pltpu.make_async_copy(w2_far, w2_ref, sem)
-    copy.start()
+def convolutions(nvar, read, total, weights_ref, bias_ref, window, hidden, count, write):
     states, cols = window.shape[0] - 2, window.shape[1]
     rows = window.shape[2]
     inner = hidden.shape[1]
@@ -189,7 +187,7 @@
         patches = [
             window[t + d, b : b + inner].reshape(inner * rows, 2 * LANES) for d in range(3) for b in range(3)
         ]
-        value = jnp.dot(jnp.concatenate(patches, 1), w1_ref[...], preferred_element_type=F32)
+        value = jnp.dot(jnp.concatenate(patches, 1), weights_ref[0], preferred_element_type=F32)
         value = 0.5 * (value + bias_ref[...])
         value = value * (1.0 + jnp.tanh(value))
         hidden[t + 1] = value.astype(BF16).reshape(inner, rows, value.shape[1])
@@ -199,7 +197,7 @@
         patches = [
             hidden[t + d, b : b + outer].reshape(outer * rows, 2 * LANES) for d in range(3) for b in range(3)
         ]
-        value = jnp.dot(jnp.concatenate(patches, 1), w2_ref[...], preferred_element_type=F32)
+        value = jnp.dot(jnp.concatenate(patches, 1), weights_ref[1], preferred_element_type=F32)
         low, high = value[:, :LANES], value[:, LANES:]
         lane = iota(low.shape, 1)
         mid = pltpu.roll(jnp.where(lane >= nvar, low, high), LANES - nvar, 1)
@@ -213,15 +211,21 @@
             fill(t, 0)
         if 1 <= t <= states:
             first(t - 1, 0)
-        if t == 2:
-            copy.wait()
         if t >= 2:
             carry = second(t - 2, carry)
     return carry
 
 
-def first_step_kernel(nvar, count, w2_ref, s_ref, w1_ref, bias_ref, x_ref, d_ref, sums_ref, window, hidden, w2, sem):
+def first_step_kernel(
+    nvar, count, _, far_ref, weights_ref, bias_ref, x_ref, d_ref, sums_ref, window, hidden, s_ref, moments, sems
+):
     rows = s_ref.shape[2]
+    states = s_ref.shape[0]
+    copies = [pltpu.make_async_copy(far_ref.at[:, s_ref.shape[1]], moments, sems.at[states])]
+    for t in range(states):
+        copies.append(pltpu.make_async_copy(far_ref.at[t, : s_ref.shape[1]], s_ref.at[t], sems.at[t]))
+    for copy in copies:
+        copy.start()
     wide = window.shape[1]
     outer = x_ref.shape[1]
     core = d_ref.shape[1]
@@ -229,6 +233,8 @@
     ring = (wide - outer) // 2
 
     def read(t):
+        for copy in copies[2:] if t == 1 else copies[1:2] if t == 0 else ():
+            copy.wait()
         state = s_ref[t, :wide].astype(F32).reshape(wide * rows, LANES)
         seen = s_ref[t, wide : wide + outer].astype(F32).reshape(outer * rows, LANES)
         lane = iota(state.shape, 1)
@@ -252,12 +258,13 @@
         own = x.reshape(outer, rows, LANES)[skip : skip + core]
         return acc + jnp.sum((own * own).reshape(core * rows // 8, 8, LANES), 0)
 
-    total = jnp.sum(s_ref[:, wide + outer].astype(F32).reshape(-1, LANES), 0, keepdims=True)
-    acc = convolutions(nvar, read, total, w2_ref, w1_ref, bias_ref, window, hidden, w2, sem, count, write)
+    copies[0].wait()
+    total = jnp.sum(moments[...].astype(F32).reshape(-1, LANES), 0, keepdims=True)
+    acc = convolutions(nvar, read, total, weights_ref, bias_ref, window, hidden, count, write)
     sums_ref[...] = jnp.broadcast_to(jnp.sum(acc, 0, keepdims=True), sums_ref.shape)
 
 
-def second_step_kernel(nvar, count, w2_ref, x_ref, d_ref, parts_ref, w1_ref, bias_ref, out_ref, window, hidden, w2, sem):
+def second_step_kernel(nvar, count, x_ref, d_ref, parts_ref, weights_ref, bias_ref, out_ref, window, hidden):
     wide, rows = x_ref.shape[1], x_ref.shape[2]
     core = d_ref.shape[1]
 
@@ -273,7 +280,7 @@
         return acc
 
     total = jnp.sum(parts_ref[...], 0, keepdims=True)
-    convolutions(nvar, read, total, w2_ref, w1_ref, bias_ref, window, hidden, w2, sem, count, write)
+    convolutions(nvar, read, total, weights_ref, bias_ref, window, hidden, count, write)
 
 
 def finish_kernel(nvar, d_ref, base_ref, out_ref, both):
@@ -324,9 +331,9 @@
     down = [(j, i) for i, j in up]
     left = lax.ppermute(packed[cols - wide :], LON, up)
     right = lax.ppermute(packed[:wide], LON, down)
-    w1, w2 = call(
+    (weights,) = call(
         functools.partial(weights_kernel, nvar),
-        [sds((9 * hid, hid), BF16), sds((9 * hid, hid), BF16)],
+        [sds((2, 9 * hid, hid), BF16)],
         [pltpu.VMEM((hid, hid), F32), pltpu.VMEM(first_weight.shape[::-1], F32)],
         first_weight.T,
         second_weight,
@@ -343,37 +350,36 @@
     )
     got = lax.all_to_all(sent, TRAJ, 0, 0)
     (base,) = call(functools.partial(base_kernel, nvar), [sds(band, F32)], scratch, *source, done, far=4)
-    w2 = pltpu.with_memory_space_constraint(w2, pltpu.HBM)
-
     def buffers(cols):
         return [
             pltpu.VMEM((parts + 2, cols, rows, hid), BF16),
             pltpu.VMEM((parts + 2, cols - 2, rows, hid), BF16),
-            pltpu.VMEM(w2.shape, BF16),
-            pltpu.SemaphoreType.DMA(()),
         ]
 
     x1, d1, sums1 = call(
         functools.partial(first_step_kernel, nvar, count),
         [sds((parts, each + 4, rows, LANES), F32), sds((parts, each, rows, LANES), F32), everyone],
-        buffers(each + 8),
-        w2,
-        got,
-        w1,
+        buffers(each + 8)
+        + [
+            pltpu.VMEM((parts, sent.shape[1] - 1, rows, LANES), BF16),
+            pltpu.VMEM((parts, rows, LANES), BF16),
+            pltpu.SemaphoreType.DMA((parts + 1,)),
+        ],
+        base,
+        pltpu.with_memory_space_constraint(got, pltpu.HBM),
+        weights,
         bias,
-        far=1,
+        far=2,
     )
     (d2,) = call(
         functools.partial(second_step_kernel, nvar, count),
         [sds((parts, each, rows, LANES), BF16)],
         buffers(each + 4),
-        w2,
         x1,
         d1,
         exchanged(sums1, ALL),
-        w1,
+        weights,
         bias,
-        far=1,
     )
     back = lax.all_to_all(d2, TRAJ, 0, 0)
     (out,) = call(

time: 91.9 us -> 92 us (level)
  blocking collectives: 22.6 us -> 39 us
  waiting for transfers between devices: 26.7 us -> 17.3 us
  starting transfers between devices: 15.1 us -> 11.2 us
  local copies, waits for them, and re-layouts: 3.53 us -> 1.25 us
    all_to_all x0 -> x1, blocking collectives: none -> 14.4 us  [body(): back = lax.all_to_all(d2, TRAJ, 0, 0)]
    all_to_all x1 -> x0, waiting for transfers between devices: 9.5 us -> none  [body(): back = lax.all_to_all(d2, TRAJ, 0, 0)]
    all_to_all x1 -> x0, starting transfers between devices: 3.51 us -> none  [body(): back = lax.all_to_all(d2, TRAJ, 0, 0)]
    unnamed x8 -> x6, local copies, waits for them, and re-layouts: 3.52 us -> 1.24 us
    all_to_all x2, blocking collectives: 22.6 us -> 24.6 us  [exchanged(): return lax.all_to_all(rows[:, None, :], axes, 0, 0)[:, 0, :]]
  transfers between devices with their start and end apart: 4 -> 3, of which waited for: 2 -> 1; matrix products, arithmetic and copies ran while one was open for 0% -> 0% of each run, Pallas kernels for 4% -> 4%
where the time goes in v2:
time: 92 us; the launch traced here: 91.7 us
  blocking collectives  39 us (42%)
  Pallas kernels  22.9 us (25%)
  waiting for transfers between devices  17.3 us (19%)
  starting transfers between devices  11.2 us (12%)
  local copies, waits for them, and re-layouts  1.25 us (1%)
    all_to_all x2, blocking collectives, exchanged(): return lax.all_to_all(rows[:, None, :], axes, 0, 0)[:, 0, :]  24.6 us
    pallas_call x7, Pallas kernels, call(): pl.pallas_call(kernel, out_shape=outs, in_specs=[pl.BlockSpec(memory_spac...  22.9 us
    all_to_all x1, waiting for transfers between devices, body(): got = lax.all_to_all(sent, TRAJ, 0, 0)  17.3 us
    all_to_all x1, blocking collectives, body(): back = lax.all_to_all(d2, TRAJ, 0, 0)  14.4 us
    all_to_all x1, starting transfers between devices, body(): got = lax.all_to_all(sent, TRAJ, 0, 0)  7.78 us
    ppermute x1, starting transfers between devices, body(): right = lax.ppermute(packed[:wide], LON, down)  3.38 us
  transfers between devices with their start and end apart: 3, of which 1 were waited for; matrix products, arithmetic and copies ran while one was open for 0% of the time, Pallas kernels for 4%

profile of v2, /device:TPU:0, one launch (start us, length us, event | category | flops | bytes accessed | tf_op | source)
XLA Modules:
  0.0 91.7 jit_solution(16125084068824121539)
XLA Ops:
  0.0 2.6 %prepare_kernel.1 = (bf16[128,32,128]{2,1,0:T(8,128)(2,1)S(1)}, f32[16,128]{1,0:T(8,128)S(1)}) custom-call(f32[1248,128]{1,0:T(8,128)} %bitcast.22, s32[1,256]{1,0:T(1,128)} %index_ref.3, f32[78,1,256]{2,1,0:T(1,128)} %bitcast.24), custom_call_target="tpu_custom_call" | custom-call | tf_op jit(solution)/shard_map/prepare_kernel/pallas_call | solution.py:22
  2.6 3.4 %collective-permute-start.1 = (bf16[4,32,128]{2,1,0:T(8,128)(2,1)S(1)}, bf16[4,32,128]{2,1,0:T(8,128)(2,1)S(1)}, u32[]{:S(2)}, u32[]{:S(2)}) collective-permute-start(bf16[4,32,128]{2,1,0:T(8,128)(2,1)S(1)} %get-tuple-element.19), channel_id=1, source_target_pairs={{1,0},{2,1},{3,2},{4,3},{5,4},{6,5},{7,6},{8,7},{9,8},{10,9},{11,1... | collective-permute-start | bytes 98312 | tf_op jit(solution)/shard_map/ppermute | solution.py:333
  6.0 0.0 collective-permute-start
  6.0 11.1 %all_to_all.20 = f32[16,1,128]{2,1,0:T(1,128)S(1)} all-to-all(f32[16,1,128]{2,1,0:T(1,128)S(1)} %bitcast.19), channel_id=1, replica_groups=mesh['traj_0'=4,'traj_1'=2,'lon_0'=2,'lon_1'=4,'lon_2'=2] {'lon_0','lon_..., dimensions={0} | all-to-all | bytes 16384 | tf_op jit(solution)/shard_map/all_to_all | solution.py:298
  17.1 0.0 collective-permute-done.1.right_ref
  17.1 0.0 collective-permute-done.left_ref
  17.1 1.3 %assemble_kernel.1 = (bf16[8,45,16,128]{3,2,1,0:T(8,128)(2,1)}, f32[8,128]{1,0:T(8,128)S(1)}) custom-call(bf16[128,32,128]{2,1,0:T(8,128)(2,1)S(1)} %get-tuple-element.12.x_ref, bf16[4,32,128]{2,1,0:T(8,128)(2,1)S(1)} %collective-permute-done.left_ref, bf16[4,32,128]{2,1,0:T(8,128)(2,1)S(1)} %collective-permute-done.1.right_ref, f32[16,128]{1,0:T(8,128)S(1)} %bitcast.18), custom_call_target="tpu_custom_call" | custom-call | tf_op jit(solution)/shard_map/assemble_kernel/pallas_call | solution.py:22
  18.4 0.0 copy-start
  18.4 7.8 %all-to-all-start.1 = ((bf16[8,45,16,128]{3,2,1,0:T(8,128)(2,1)}), bf16[8,45,16,128]{3,2,1,0:T(8,128)(2,1)}, u32[]{:S(2)}, u32[]{:S(2)}) async-start(bf16[8,45,16,128]{3,2,1,0:T(8,128)(2,1)} %get-tuple-element.15), calls=%async_computation.1 | async-start | bytes 2949120 | tf_op jit(solution)/shard_map/all_to_all | solution.py:351
  26.2 0.0 copy-done
  26.2 0.0 copy-start.1
  26.2 1.2 %copy-done.1 = bf16[256,2106]{0,1:T(8,128)(2,1)S(1)} copy-done((bf16[256,2106]{0,1:T(8,128)(2,1)S(1)}, bf16[256,2106]{0,1:T(8,128)(2,1)}, u32[]{:S(2)}) %copy-start.1) | copy-done | bytes 1078296
  27.4 1.1 %weights_kernel.1.weights_ref = bf16[2,2304,256]{2,1,0:T(8,128)(2,1)S(1)} custom-call(bf16[2106,256]{1,0:T(8,128)(2,1)S(1)} %bitcast.15, bf16[234,2304]{1,0:T(8,128)(2,1)S(1)} %copy-done), custom_call_target="tpu_custom_call" | custom-call | tf_op jit(solution)/shard_map/weights_kernel/pallas_call | solution.py:22
  28.5 0.0 copy-start.2
  28.5 2.2 %base_kernel.1._.base_ref = f32[128,16,128]{2,1,0:T(8,128)S(1)} custom-call(f32[1248,128]{1,0:T(8,128)} %bitcast.23, s32[1,256]{1,0:T(1,128)} %index_ref.3, f32[78,1,256]{2,1,0:T(1,128)} %bitcast.25, f32[8,128]{1,0:T(8,128)S(1)} %get-tuple-element.14.after_ref), custom_call_target="tpu_custom_call" | custom-call | tf_op jit(solution)/shard_map/base_kernel/pallas_call | solution.py:22
  30.7 17.3 %all-to-all-done.1.far_ref = bf16[8,45,16,128]{3,2,1,0:T(8,128)(2,1)} async-done(((bf16[8,45,16,128]{3,2,1,0:T(8,128)(2,1)}), bf16[8,45,16,128]{3,2,1,0:T(8,128)(2,1)}, u32[]{:S(2)}, u32[]{:S(2)}) %all-to-all-start.1) | async-done | bytes 1474592 | tf_op jit(solution)/shard_map/all_to_all | solution.py:351
  48.1 0.0 copy-done.2
  48.1 8.5 %first_step_kernel.1 = (f32[8,20,16,128]{3,2,1,0:T(8,128)S(1)}, f32[8,16,16,128]{3,2,1,0:T(8,128)S(1)}, f32[128,128]{1,0:T(8,128)S(1)}) custom-call(f32[128,16,128]{2,1,0:T(8,128)S(1)} %base_kernel.1._.base_ref, bf16[8,45,16,128]{3,2,1,0:T(8,128)(2,1)} %all-to-all-done.1.far_ref, bf16[2,2304,256]{2,1,0:T(8,128)(2,1)S(1)} %weights_kernel.1.weights_ref, ...), custom_call_target="tpu_custom_call" | custom-call | tf_op jit(solution)/shard_map/first_step_kernel/pallas_call | solution.py:22
  56.6 13.5 %all_to_all.21 = f32[128,1,128]{2,1,0:T(1,128)S(1)} all-to-all(f32[128,1,128]{2,1,0:T(1,128)S(1)} %bitcast.17), channel_id=1, replica_groups=mesh['traj_0'=4,'traj_1'=2,'lon_0'=2,'lon_1'=4,'lon_2'=2] {'traj_0','tra..., dimensions={0} | all-to-all | bytes 131072 | tf_op jit(solution)/shard_map/all_to_all | solution.py:298
  70.0 5.7 %second_step_kernel.1 = bf16[8,16,16,128]{3,2,1,0:T(8,128)(2,1)S(1)} custom-call(f32[8,20,16,128]{3,2,1,0:T(8,128)S(1)} %get-tuple-element.16.x_ref, f32[8,16,16,128]{3,2,1,0:T(8,128)S(1)} %get-tuple-element.17.d_ref, f32[128,128]{1,0:T(8,128)S(1)} %bitcast.16, bf16[2,2304,256]{2,1,0:T(8,128)(2,1)S(1)} %weights_kernel.1.weights_ref, f32[1,256]{1,0:T(1,128)S(1)} %bitcast.21), custom_call_target="tpu_custom_call" | custom-call | tf_op jit(solution)/shard_map/second_step_kernel/pallas_call | solution.py:22
  75.7 14.4 %all_to_all.22 = bf16[8,16,16,128]{3,2,1,0:T(8,128)(2,1)S(1)} all-to-all(bf16[8,16,16,128]{3,2,1,0:T(8,128)(2,1)S(1)} %second_step_kernel.1), channel_id=1, replica_groups=mesh['traj_0'=4,'traj_1'=2,'lon_0'=2,'lon_1'=4,'lon_2'=2] {'traj_0','tra..., dimensions={0} | all-to-all | bytes 1048576 | tf_op jit(solution)/shard_map/all_to_all | solution.py:384
  90.1 1.6 %finish_kernel.1 = f32[1248,128]{1,0:T(8,128)} custom-call(bf16[128,16,128]{2,1,0:T(8,128)(2,1)S(1)} %bitcast.14, f32[128,16,128]{2,1,0:T(8,128)S(1)} %base_kernel.1._.base_ref), custom_call_target="tpu_custom_call" | custom-call | tf_op jit(solution)/shard_map/finish_kernel/pallas_call | solution.py:22
  (1 shorter events, 0.0 us)
Async XLA Ops:
  2.6 14.5 %collective-permute-start.1 = (bf16[4,32,128]{2,1,0:T(8,128)(2,1)S(1)}, bf16[4,32,128]{2,1,0:T(8,128)(2,1)S(1)}, u32[]{:S(2)}, u32[]{:S(2)}) collective-permute-start(bf16[4,32,128]{2,1,0:T(8,128)(2,1)S(1)} %get-tuple-element.19), channel_id=1, source_target_pairs={{1,0},{2,1},{3,2},{4,3},{5,4},{6,5},{7,6},{8,7},{9,8},{10,9},{11,1... | collective-permute-start | bytes 98312 | tf_op jit(solution)/shard_map/ppermute | solution.py:333
  6.0 11.1 %collective-permute-start = (bf16[4,32,128]{2,1,0:T(8,128)(2,1)S(1)}, bf16[4,32,128]{2,1,0:T(8,128)(2,1)S(1)}, u32[]{:S(2)}, u32[]{:S(2)}) collective-permute-start(bf16[4,32,128]{2,1,0:T(8,128)(2,1)S(1)} %get-tuple-element.20), channel_id=1, source_target_pairs={{0,1},{1,2},{2,3},{3,4},{4,5},{5,6},{6,7},{7,8},{8,9},{9,10},{10,1... | collective-permute-start | bytes 98312 | tf_op jit(solution)/shard_map/ppermute | solution.py:332
  18.4 7.8 %copy-start = (bf16[234,2304]{1,0:T(8,128)(2,1)S(1)}, bf16[234,2304]{1,0:T(8,128)(2,1)}, u32[]{:S(2)}) copy-start(bf16[234,2304]{1,0:T(8,128)(2,1)} %w2_ref.1) | copy-start | bytes 3234820
  18.4 29.7 %all-to-all-start.1 = ((bf16[8,45,16,128]{3,2,1,0:T(8,128)(2,1)}), bf16[8,45,16,128]{3,2,1,0:T(8,128)(2,1)}, u32[]{:S(2)}, u32[]{:S(2)}) async-start(bf16[8,45,16,128]{3,2,1,0:T(8,128)(2,1)} %get-tuple-element.15), calls=%async_computation.1 | async-start | bytes 2949120 | tf_op jit(solution)/shard_map/all_to_all | solution.py:351
  26.2 1.2 %copy-start.1 = (bf16[256,2106]{0,1:T(8,128)(2,1)S(1)}, bf16[256,2106]{0,1:T(8,128)(2,1)}, u32[]{:S(2)}) copy-start(bf16[256,2106]{0,1:T(8,128)(2,1)} %param.9) | copy-start | bytes 3234820
  28.5 19.6 %copy-start.2 = (f32[256]{0:T(256)S(1)}, f32[256]{0:T(256)}, u32[]{:S(2)}) copy-start(f32[256]{0:T(256)} %param.10) | copy-start | bytes 3076
